TPU v7x, 32 devices: a whole 2x2x4 slice. The times are simulated.
32 devices in a mesh: dp: 16 (over z, x, core), mp: 2 (over y).
Axes of the slice: x: 2, y: 2, z: 4, core: 2. Of those that a mesh axis runs over, the one named last changes fastest.
Arguments:
- context: bfloat16 [5120, 2048], P('dp', 'mp'), may hold values from -6 to 6
- out_weight: bfloat16 [2048, 3584], P('mp'), may hold values from -0.125 to 0.125
- cotangent: bfloat16 [5120, 3584], P('dp'), may hold values from -0.059814453 to 0.059814453
- norm_gain: float32 [3584], replicated, may hold values from 0.5 to 1.5
- first_moment: float32 [2, 1024, 3584], P('mp', 'dp'), may hold values from -6 to 6
- second_moment: float32 [2, 1024, 3584], P('mp', 'dp'), may hold values from 0.01 to 1
Outputs:
- new_weight: bfloat16 [2, 1024, 3584], P('mp', 'dp')
- new_first: float32 [2, 1024, 3584], P('mp', 'dp')
- new_second: float32 [2, 1024, 3584], P('mp', 'dp')
- grad_gain: float32 [3584], replicated
- grad_context: bfloat16 [5120, 2048], P('dp', 'mp')
All inputs are finite; a program needn't handle non-finite values.
Results may differ from a plain program's by a relative error of at most 0.005.
Values may be sent and summed in bfloat16 or wider, within the bound.
A program may use at most 128 MiB of HBM per device.

v0:
```python
import jax
import jax.numpy as jnp
from jax import lax
from jax.sharding import PartitionSpec as P

norm_floor = 0.1
learn_rate = 0.01
beta_one = 0.9
beta_two = 0.95
adam_floor = 1e-08


def adam_update(master, first_moment, second_moment, grad_shard):
    new_first = beta_one * first_moment + (1.0 - beta_one) * grad_shard
    new_second = beta_two * second_moment + (1.0 - beta_two) * grad_shard * grad_shard
    new_weight = (master - learn_rate * new_first / (jnp.sqrt(new_second) + adam_floor)).astype(
        jnp.bfloat16
    )
    return (new_weight, new_first, new_second)


def per_device(context, out_weight, cotangent, norm_gain, first_moment, second_moment):
    width = out_weight.shape[1]
    partial_value = jnp.dot(context, out_weight, preferred_element_type=jnp.float32)
    half_width = width // lax.axis_size("mp")
    offset = lax.axis_index("mp") * half_width
    attn_half = lax.psum_scatter(partial_value, "mp", scatter_dimension=1, tiled=True)
    gain_half = lax.dynamic_slice_in_dim(norm_gain, offset, half_width, 0)
    upstream = lax.dynamic_slice_in_dim(cotangent, offset, half_width, 1).astype(jnp.float32)
    squares = jnp.sum(attn_half * attn_half, axis=-1, keepdims=True)
    total_sq = lax.psum(squares, "mp")
    inverse = lax.rsqrt(total_sq / width + norm_floor)
    normed = attn_half * inverse
    scaled = upstream * gain_half
    product_half = jnp.sum(scaled * normed, axis=-1, keepdims=True)
    product_all = lax.psum(product_half, "mp")
    grad_half = (inverse * (scaled - normed * (product_all / width))).astype(jnp.bfloat16)
    grad_attn = lax.all_gather(grad_half, "mp", axis=1, tiled=True)
    gain_part = jnp.sum(upstream * normed, axis=0)
    gain_total = lax.psum(gain_part, "dp")
    grad_gain = lax.all_gather(gain_total, "mp", axis=0, tiled=True)
    shard_rows = first_moment.shape[1]
    master = lax.dynamic_slice_in_dim(
        out_weight, lax.axis_index("dp") * shard_rows, shard_rows, 0
    ).astype(jnp.float32)[None]
    grad_shard = lax.psum_scatter(
        lax.dot_general(
            context, grad_attn, (((0,), (0,)), ((), ())), preferred_element_type=jnp.float32
        ),
        "dp",
        scatter_dimension=0,
        tiled=True,
    )
    grad_context = lax.dot_general(
        grad_attn, out_weight, (((1,), (1,)), ((), ())), preferred_element_type=jnp.float32
    ).astype(jnp.bfloat16)
    new_weight, new_first, new_second = adam_update(
        master, first_moment, second_moment, grad_shard[None]
    )
    return (new_weight, new_first, new_second, grad_gain, grad_context)


def solution(mesh):
    return jax.shard_map(
        per_device,
        mesh=mesh,
        in_specs=(
            P("dp", "mp"),
            P("mp", None),
            P("dp", None),
            P(),
            P("mp", "dp", None),
            P("mp", "dp", None),
        ),
        out_specs=(
            P("mp", "dp", None),
            P("mp", "dp", None),
            P("mp", "dp", None),
            P(),
            P("dp", "mp"),
        ),
        check_vma=False,
    )
```

profile of v0, /device:TPU:0, one launch (start us, length us, event | category | flops | bytes accessed | tf_op | source)
XLA Modules:
  0.0 323.5 jit_solution(9615545915211681465)
XLA Ops:
  7.2 1.0 copy-done
  8.3 7.7 %fusion.10 = f32[320,3584]{1,0:T(8,128)} fusion(bf16[320,1024]{1,0:T(8,128)(2,1)S(1)} %copy-done, bf16[1024,3584]{1,0:T(8,128)(2,1)} %param.7), kind=kOutput, calls=%fused_computation.20 | convolution fusion | flops 2348810240 | bytes 12582912 | tf_op jit(solution)/shard_map/dot_general | solution.py:24
  16.0 0.6 copy-done.5
  16.7 60.8 %reduce-scatter.5.cloned.1.call-done = f32[320,1792]{1,0:T(8,128)} async-done(((f32[320,3584]{1,0:T(8,128)}), f32[320,1792]{1,0:T(8,128)}) %reduce-scatter.5.cloned.1.call-update) | async-done | bytes 2293776 | tf_op jit(solution)/shard_map/reduce_scatter | solution.py:27
  77.5 2.0 multiply_reduce_fusion
  79.5 4.9 %psum.21 = f32[320,1]{0,1:T(1,128)S(1)} all-reduce(f32[320,1]{0,1:T(1,128)S(1)} %broadcast_in_dim.16), channel_id=1, replica_groups=mesh['dp'=16,'mp'=2] {'mp'}, use_global_device_ids=true, to_apply=%region_2.0 | all-reduce | flops 320 | bytes 2560 | tf_op jit(solution)/shard_map/psum | solution.py:31
  84.5 2.1 fusion.5
  86.6 4.9 %psum.22 = f32[320,1]{0,1:T(1,128)S(1)} all-reduce(f32[320,1]{0,1:T(1,128)S(1)} %broadcast_in_dim.17), channel_id=1, replica_groups=mesh['dp'=16,'mp'=2] {'mp'}, use_global_device_ids=true, to_apply=%region_4.0 | all-reduce | flops 320 | bytes 2560 | tf_op jit(solution)/shard_map/psum | solution.py:36
  91.5 2.8 fusion.4
  94.4 35.4 %all-gather.3.cloned.1.call-done = bf16[320,3584]{1,0:T(8,128)(2,1)} async-done(((bf16[320,1792]{1,0:T(8,128)(2,1)}), bf16[320,3584]{1,0:T(8,128)(2,1)}) %all-gather.3.cloned.1.call-update) | async-done | bytes 2293776 | tf_op jit(solution)/shard_map/all_gather | solution.py:38
  129.8 8.9 %convolution_bitcast_fusion = f32[1024,3584]{0,1:T(8,128)} fusion(bf16[320,3584]{1,0:T(8,128)(2,1)} %all-gather.3.cloned.1.call-done, bf16[320,1024]{1,0:T(8,128)(2,1)S(1)} %copy-done), kind=kOutput, calls=%fused_computation | convolution fusion | flops 2348810240 | bytes 17629184 | tf_op jit(solution)/shard_map/dot_general | solution.py:47
  138.8 14.3 %copy.29 = f32[1024,3584]{1,0:T(8,128)} copy(f32[1024,3584]{0,1:T(8,128)} %convolution_bitcast_fusion) | data formatting | bytes 29360128
  153.1 1.1 constant_dynamic-slice_fusion
  154.6 1.7 copy.24
  156.4 3.0 copy.25
  159.3 33.6 %psum.23 = f32[1792]{0:T(1024)S(1)} all-reduce(f32[1792]{0:T(1024)S(1)} %get-tuple-element.20), channel_id=1, replica_groups=mesh['dp'=16,'mp'=2] {'dp'}, use_global_device_ids=true, to_apply=%region_7.0 | all-reduce | flops 1792 | bytes 14336 | tf_op jit(solution)/shard_map/psum | solution.py:40
  192.9 4.4 %all-gather = f32[2,1,1792]{2,1,0:T(1,128)S(1)} all-gather(f32[1,1,1792]{2,1,0:T(1,128)S(1)} %reshape.15), channel_id=1, replica_groups=mesh['dp'=16,'mp'=2] {'mp'}, dimensions={0}, use_global_device_ids=true | all-gather | bytes 21504 | tf_op jit(solution)/shard_map/all_gather | solution.py:41
  198.0 7.3 %convolution_convert_fusion = bf16[320,1024]{1,0:T(8,128)(2,1)} fusion(bf16[320,3584]{1,0:T(8,128)(2,1)} %all-gather.3.cloned.1.call-done, bf16[1024,3584]{1,0:T(8,128)(2,1)} %param.7), kind=kOutput, calls=%fused_computation.16 | convolution fusion | flops 2349137920 | bytes 10289152 | tf_op jit(solution)/shard_map/dot_general | solution.py:54
  205.3 98.2 %reduce-scatter.7.cloned.1.call-done = f32[64,3584]{1,0:T(8,128)} async-done(((f32[1024,3584]{1,0:T(8,128)}), f32[64,3584]{1,0:T(8,128)}) %reduce-scatter.7.cloned.1.call-update) | async-done | bytes 917520
  303.4 3.0 copy.30
  306.4 4.9 %fusion.8 = (bf16[1,64,3584]{1,2,0:T(8,128)(2,1)}, f32[1,64,3584]{1,2,0:T(8,128)}, f32[1,64,3584]{1,2,0:T(8,128)}) fusion(bf16[64,3584]{0,1:T(8,128)(2,1)S(1)} %copy.31, f32[64,3584]{0,1:T(8,128)} %copy.30, f32[1,64,3584]{1,2,0:T(8,128)S(1)} %copy.24, f32[1,64,3584]{1,2,0:T(8,128)} %copy.25), kind=kLoop, calls=%fused_computation.14 | loop fusion | flops 2981888 | bytes 5505024 | tf_op jit(solution)/shard_map/convert_element_type | solution.py:16
  311.3 3.1 copy.27
  314.4 1.4 copy.28
  315.9 1.1 copy.26
  (25 shorter events, 1.4 us)
Async XLA Ops:
  7.2 1.1 copy-start
  7.2 70.3 %reduce-scatter.5.cloned.1.call-start = ((), (), s32[]{:S(2)}) async-start(), calls=%async_computation.2 | async-start | bytes 6881280 | tf_op jit(solution)/shard_map/reduce_scatter | solution.py:27
  15.9 0.7 copy-start.5
  16.0 113.9 %all-gather.3.cloned.1.call-start = ((), (), s32[]{:S(2)}) async-start(), calls=%async_computation.3 | async-start | bytes 3440640 | tf_op jit(solution)/shard_map/all_gather | solution.py:38
  77.5 7.0 %copy-start.2 = (f32[320,1792]{1,0:T(8,128)S(1)}, f32[320,1792]{1,0:T(8,128)}, u32[]{:S(2)}) copy-start(f32[320,1792]{1,0:T(8,128)} %reduce-scatter.5.cloned.1.call-done) | copy-start | bytes 6881284
  94.4 209.1 %reduce-scatter.7.cloned.1.call-start = ((), (), s32[]{:S(2)}) async-start(), calls=%async_computation.4 | async-start | bytes 15597568
  311.3 3.1 copy-start.3
  311.3 4.5 %copy-start.4 = (bf16[1,64,3584]{1,2,0:T(8,128)(2,1)S(1)}, bf16[1,64,3584]{1,2,0:T(8,128)(2,1)}, u32[]{:S(2)}) copy-start(bf16[1,64,3584]{1,2,0:T(8,128)(2,1)} %get-tuple-element.22) | copy-start | bytes 1376260
  311.3 5.6 %copy-start.1 = (bf16[320,1024]{1,0:T(8,128)(2,1)S(1)}, bf16[320,1024]{1,0:T(8,128)(2,1)}, u32[]{:S(2)}) copy-start(bf16[320,1024]{1,0:T(8,128)(2,1)} %param.6) | copy-start | bytes 1966084
Sparse Core Ops, SparseCore 0:
  16.1 61.3 reduce-scatter.4
  94.5 35.3 all-gather.2
  153.3 150.1 reduce-scatter.6
where the time goes:
time: 324 us; the launch traced here: 323 us
  waiting for transfers between devices  194 us (60%)
  blocking collectives  47.8 us (15%)
  local copies, waits for them, and re-layouts  31.5 us (10%)
  matrix products  23.9 us (7%)
  between operations  13.8 us (4%)
  other arithmetic  11.9 us (4%)
    unnamed x4, waiting for transfers between devices  98.2 us
    reduce_scatter x1, waiting for transfers between devices, per_device(): lax.psum_scatter(partial_value, 'mp', scatter_dimension=1, tiled=True)  60.8 us
    all_gather x1, waiting for transfers between devices, per_device(): grad_attn = lax.all_gather(grad_half, 'mp', axis=1, tiled=True)  35.4 us
    psum x1, blocking collectives, per_device(): gain_total = lax.psum(gain_part, 'dp')  33.6 us
    unnamed x22, local copies, waits for them, and re-layouts  30.3 us
    dot_general x1, matrix products, per_device(): lax.dot_general(context, grad_attn, (((0,), (0,)), ((), ())), preferred_e...  8.95 us
    dot_general x1, matrix products, per_device(): jnp.dot(context, out_weight, preferred_element_type=jnp.float32)  7.67 us
    dot_general x1, matrix products, per_device(): lax.dot_general(grad_attn, out_weight, (((1,), (1,)), ((), ())), preferre...  7.26 us
  transfers between devices with their start and end apart: 3, of which 3 were waited for; matrix products, arithmetic and copies ran while one was open for 4% of the time, Pallas kernels for 0%

commit v1 on v0

--- a/solution.py
+++ b/solution.py
@@ -37,7 +37,8 @@
     grad_half = (inverse * (scaled - normed * (product_all / width))).astype(jnp.bfloat16)
     grad_attn = lax.all_gather(grad_half, "mp", axis=1, tiled=True)
     gain_part = jnp.sum(upstream * normed, axis=0)
-    gain_total = lax.psum(gain_part, "dp")
+    pieces = lax.all_gather(gain_part, "dp", axis=0, tiled=False)
+    gain_total = pieces.sum(axis=0)
     grad_gain = lax.all_gather(gain_total, "mp", axis=0, tiled=True)
     shard_rows = first_moment.shape[1]
     master = lax.dynamic_slice_in_dim(

time: 324 us -> 324 us (level)
  waiting for transfers between devices: 194 us -> 206 us
  blocking collectives: 47.8 us -> 35.9 us
    psum x1 -> x0, blocking collectives: 33.6 us -> none  [per_device(): gain_total = lax.psum(gain_part, 'dp')]
    all_gather x0 -> x1, blocking collectives: none -> 21.6 us  [per_device(): pieces = lax.all_gather(gain_part, 'dp', axis=0, tiled=False)]
    unnamed x4, waiting for transfers between devices: 98.2 us -> 109 us
    unnamed x22 -> x23, local copies, waits for them, and re-layouts: 30.3 us -> 30.3 us
  transfers between devices with their start and end apart: 3 -> 3, of which waited for: 3 -> 3; matrix products, arithmetic and copies ran while one was open for 4% -> 5% of each run, Pallas kernels for 0% -> 0%
where the time goes in v1:
time: 324 us; the launch traced here: 323 us
  waiting for transfers between devices  206 us (64%)
  blocking collectives  35.9 us (11%)
  local copies, waits for them, and re-layouts  31.5 us (10%)
  matrix products  24.5 us (8%)
  between operations  13.8 us (4%)
  other arithmetic  12 us (4%)
    unnamed x4, waiting for transfers between devices  109 us
    reduce_scatter x1, waiting for transfers between devices, per_device(): lax.psum_scatter(partial_value, 'mp', scatter_dimension=1, tiled=True)  60.8 us
    all_gather x1, waiting for transfers between devices, per_device(): grad_attn = lax.all_gather(grad_half, 'mp', axis=1, tiled=True)  35.4 us
    unnamed x23, local copies, waits for them, and re-layouts  30.3 us
    all_gather x1, blocking collectives, per_device(): pieces = lax.all_gather(gain_part, 'dp', axis=0, tiled=False)  21.6 us
    dot_general x1, matrix products, per_device(): lax.dot_general(context, grad_attn, (((0,), (0,)), ((), ())), preferred_e...  8.95 us
    dot_general x1, matrix products, per_device(): lax.dot_general(grad_attn, out_weight, (((1,), (1,)), ((), ())), preferre...  7.86 us
    dot_general x1, matrix products, per_device(): jnp.dot(context, out_weight, preferred_element_type=jnp.float32)  7.67 us
  transfers between devices with their start and end apart: 3, of which 3 were waited for; matrix products, arithmetic and copies ran while one was open for 5% of the time, Pallas kernels for 0%

profile of v1, /device:TPU:0, one launch (start us, length us, event | category | flops | bytes accessed | tf_op | source)
XLA Modules:
  0.0 323.4 jit_solution(14765775029541897819)
XLA Ops:
  7.2 1.0 copy-done
  8.3 7.7 %fusion.10 = f32[320,3584]{1,0:T(8,128)} fusion(bf16[320,1024]{1,0:T(8,128)(2,1)S(1)} %copy-done, bf16[1024,3584]{1,0:T(8,128)(2,1)} %param.7), kind=kOutput, calls=%fused_computation.20 | convolution fusion | flops 2348810240 | bytes 12582912 | tf_op jit(solution)/shard_map/dot_general | solution.py:24
  16.0 0.6 copy-done.5
  16.7 60.8 %reduce-scatter.5.cloned.1.call-done = f32[320,1792]{1,0:T(8,128)} async-done(((f32[320,3584]{1,0:T(8,128)}), f32[320,1792]{1,0:T(8,128)}) %reduce-scatter.5.cloned.1.call-update) | async-done | bytes 2293776 | tf_op jit(solution)/shard_map/reduce_scatter | solution.py:27
  77.5 2.0 multiply_reduce_fusion
  79.5 4.9 %psum.14 = f32[320,1]{0,1:T(1,128)S(1)} all-reduce(f32[320,1]{0,1:T(1,128)S(1)} %broadcast_in_dim.16), channel_id=1, replica_groups=mesh['dp'=16,'mp'=2] {'mp'}, use_global_device_ids=true, to_apply=%region_2.0 | all-reduce | flops 320 | bytes 2560 | tf_op jit(solution)/shard_map/psum | solution.py:31
  84.5 2.1 fusion.5
  86.6 4.9 %psum.15 = f32[320,1]{0,1:T(1,128)S(1)} all-reduce(f32[320,1]{0,1:T(1,128)S(1)} %broadcast_in_dim.17), channel_id=1, replica_groups=mesh['dp'=16,'mp'=2] {'mp'}, use_global_device_ids=true, to_apply=%region_4.0 | all-reduce | flops 320 | bytes 2560 | tf_op jit(solution)/shard_map/psum | solution.py:36
  91.5 2.8 fusion.4
  94.4 35.4 %all-gather.5.cloned.1.call-done = bf16[320,3584]{1,0:T(8,128)(2,1)} async-done(((bf16[320,1792]{1,0:T(8,128)(2,1)}), bf16[320,3584]{1,0:T(8,128)(2,1)}) %all-gather.5.cloned.1.call-update) | async-done | bytes 2293776 | tf_op jit(solution)/shard_map/all_gather | solution.py:38
  129.8 8.9 %convolution_bitcast_fusion = f32[1024,3584]{0,1:T(8,128)} fusion(bf16[320,3584]{1,0:T(8,128)(2,1)} %all-gather.5.cloned.1.call-done, bf16[320,1024]{1,0:T(8,128)(2,1)S(1)} %copy-done), kind=kOutput, calls=%fused_computation | convolution fusion | flops 2348810240 | bytes 17629184 | tf_op jit(solution)/shard_map/dot_general | solution.py:48
  138.8 14.3 %copy.29 = f32[1024,3584]{1,0:T(8,128)} copy(f32[1024,3584]{0,1:T(8,128)} %convolution_bitcast_fusion) | data formatting | bytes 29360128
  153.1 1.1 constant_dynamic-slice_fusion
  154.6 1.7 copy.24
  156.4 3.0 copy.25
  159.3 21.6 %all-gather.1 = f32[16,1,1792]{2,1,0:T(1,128)S(1)} all-gather(f32[1,1,1792]{2,1,0:T(1,128)S(1)} %reshape.16), channel_id=2, replica_groups=mesh['dp'=16,'mp'=2] {'dp'}, dimensions={0}, use_global_device_ids=true | all-gather | bytes 121856 | tf_op jit(solution)/shard_map/all_gather | solution.py:40
  181.0 4.4 %all-gather.2 = f32[2,1,1792]{2,1,0:T(1,128)S(1)} all-gather(f32[1,1,1792]{2,1,0:T(1,128)S(1)} %reshape.18), channel_id=1, replica_groups=mesh['dp'=16,'mp'=2] {'mp'}, dimensions={0}, use_global_device_ids=true | all-gather | bytes 21504 | tf_op jit(solution)/shard_map/all_gather | solution.py:42
  186.1 7.9 %convolution_convert_fusion = bf16[320,1024]{1,0:T(8,128)(2,1)} fusion(bf16[320,3584]{1,0:T(8,128)(2,1)} %all-gather.5.cloned.1.call-done, bf16[1024,3584]{1,0:T(8,128)(2,1)} %param.7), kind=kOutput, calls=%fused_computation.16 | convolution fusion | flops 2349137920 | bytes 10289152 | tf_op jit(solution)/shard_map/dot_general | solution.py:55
  194.0 109.4 %reduce-scatter.7.cloned.1.call-done = f32[64,3584]{1,0:T(8,128)} async-done(((f32[1024,3584]{1,0:T(8,128)}), f32[64,3584]{1,0:T(8,128)}) %reduce-scatter.7.cloned.1.call-update) | async-done | bytes 917520
  303.4 3.0 copy.30
  306.4 4.9 %fusion.8 = (bf16[1,64,3584]{1,2,0:T(8,128)(2,1)}, f32[1,64,3584]{1,2,0:T(8,128)}, f32[1,64,3584]{1,2,0:T(8,128)}) fusion(bf16[64,3584]{0,1:T(8,128)(2,1)S(1)} %copy.31, f32[64,3584]{0,1:T(8,128)} %copy.30, f32[1,64,3584]{1,2,0:T(8,128)S(1)} %copy.24, f32[1,64,3584]{1,2,0:T(8,128)} %copy.25), kind=kLoop, calls=%fused_computation.14 | loop fusion | flops 2981888 | bytes 5505024 | tf_op jit(solution)/shard_map/convert_element_type | solution.py:16
  311.3 3.1 copy.27
  314.4 1.4 copy.28
  315.8 1.1 copy.26
  (27 shorter events, 1.5 us)
Async XLA Ops:
  7.2 1.1 copy-start
  7.2 70.3 %reduce-scatter.5.cloned.1.call-start = ((), (), s32[]{:S(2)}) async-start(), calls=%async_computation.2 | async-start | bytes 6881280 | tf_op jit(solution)/shard_map/reduce_scatter | solution.py:27
  15.9 0.7 copy-start.5
  16.0 113.9 %all-gather.5.cloned.1.call-start = ((), (), s32[]{:S(2)}) async-start(), calls=%async_computation.3 | async-start | bytes 3440640 | tf_op jit(solution)/shard_map/all_gather | solution.py:38
  77.5 7.0 %copy-start.2 = (f32[320,1792]{1,0:T(8,128)S(1)}, f32[320,1792]{1,0:T(8,128)}, u32[]{:S(2)}) copy-start(f32[320,1792]{1,0:T(8,128)} %reduce-scatter.5.cloned.1.call-done) | copy-start | bytes 6881284
  94.4 209.0 %reduce-scatter.7.cloned.1.call-start = ((), (), s32[]{:S(2)}) async-start(), calls=%async_computation.4 | async-start | bytes 15597568
  311.3 3.1 copy-start.3
  311.3 4.5 %copy-start.4 = (bf16[1,64,3584]{1,2,0:T(8,128)(2,1)S(1)}, bf16[1,64,3584]{1,2,0:T(8,128)(2,1)}, u32[]{:S(2)}) copy-start(bf16[1,64,3584]{1,2,0:T(8,128)(2,1)} %get-tuple-element.22) | copy-start | bytes 1376260
  311.3 5.6 %copy-start.1 = (bf16[320,1024]{1,0:T(8,128)(2,1)S(1)}, bf16[320,1024]{1,0:T(8,128)(2,1)}, u32[]{:S(2)}) copy-start(bf16[320,1024]{1,0:T(8,128)(2,1)} %param.6) | copy-start | bytes 1966084
Sparse Core Ops, SparseCore 0:
  16.1 61.3 reduce-scatter.4
  94.5 35.3 all-gather.4
  153.3 150.0 reduce-scatter.6
